TPU v7x, 32 devices: a whole 2x2x4 slice. The times are simulated.
32 devices in a mesh: tok: 16 (over z, y, x), blk: 2 (over core).
Axes of the slice: x: 2, y: 2, z: 4, core: 2. Of those that a mesh axis runs over, the one named last changes fastest.
Arguments:
- activations: bfloat16 [4096, 2048], P('tok', 'blk'), may hold values from -16 to 16
Outputs:
- factored: float32 [2048, 2048], P('blk', 'tok')
All inputs are finite; a program needn't handle non-finite values.
Results may differ from a plain program's by a relative error of at most 0.0003.
Values may be sent and summed in bfloat16 or wider, within the bound.
A program may use at most 64 MiB of HBM per device.

v0:
```python
import jax
import jax.numpy as jnp
from jax import lax
from jax.sharding import PartitionSpec as P

STEPS = 4


def spread(block, axis, holder):
    block = jnp.where(lax.axis_index(axis) == holder, block, jnp.zeros_like(block))
    return lax.psum(block, axis)


def shards(activations):
    rows_block = activations.shape[1]
    tok_count = lax.axis_size("tok")
    blk_count = lax.axis_size("blk")
    full_width = rows_block * blk_count
    strip_width = full_width // tok_count
    total_tokens = activations.shape[0] * tok_count
    partial_rows = lax.dot_general(
        activations,
        lax.all_gather(activations, "blk", axis=1, tiled=True),
        (((0,), (0,)), ((), ())),
        preferred_element_type=jnp.float32,
    )
    pieces = lax.all_to_all(partial_rows, "tok", split_axis=1, concat_axis=0, tiled=True)
    hessian_tile = jnp.sum(pieces.reshape(tok_count, rows_block, strip_width), axis=0) * (
        2.0 / total_tokens
    )
    tok_index = lax.axis_index("tok")
    blk_index = lax.axis_index("blk")
    row_ids = blk_index * rows_block + jnp.arange(rows_block, dtype=jnp.int32)[:, None]
    col_ids = tok_index * strip_width + jnp.arange(strip_width, dtype=jnp.int32)[None, :]
    on_diag = row_ids == col_ids
    trace_total = lax.psum(jnp.sum(jnp.where(on_diag, hessian_tile, 0.0)), ("tok", "blk"))
    hessian_tile = hessian_tile + jnp.where(on_diag, 0.01 * trace_total / full_width, 0.0)
    positions = jnp.arange(full_width, dtype=jnp.int32)[:, None]
    for section in range(STEPS):
        strip_rows = spread(hessian_tile, "tok", section)
        column = lax.all_gather(strip_rows, "blk", axis=0, tiled=True)
        pivot_block = column[section * strip_width : (section + 1) * strip_width]
        factor = jnp.linalg.cholesky(pivot_block)
        solved = jax.scipy.linalg.solve_triangular(factor, column.T, lower=True).T
        solved = jnp.where(positions >= section * strip_width, solved, 0.0)
        own_rows = lax.dynamic_slice_in_dim(solved, blk_index * rows_block, rows_block, 0)
        own_cols = lax.dynamic_slice_in_dim(solved, tok_index * strip_width, strip_width, 0)
        update = jnp.dot(own_rows, own_cols.T, precision=lax.Precision.HIGHEST)
        hessian_tile = jnp.where(
            tok_index > section,
            hessian_tile - update,
            jnp.where(tok_index == section, own_rows, hessian_tile),
        )
    return jnp.where(row_ids >= col_ids, hessian_tile, 0.0)


def solution(mesh):
    return jax.shard_map(
        shards,
        mesh=mesh,
        in_specs=(P("tok", "blk"),),
        out_specs=P("blk", "tok"),
        check_vma=False,
    )
```

profile of v0, /device:TPU:0, one launch (start us, length us, event | category | flops | bytes accessed | tf_op | source)
XLA Modules:
  0.0 871.7 jit_solution(5197727431388348437)
XLA Ops:
  7.3 13.4 %all-gather.6.cloned.1.call-done = bf16[256,2048]{1,0:T(8,128)(2,1)} async-done(((bf16[256,1024]{1,0:T(8,128)(2,1)}), bf16[256,2048]{1,0:T(8,128)(2,1)}) %all-gather.6.cloned.1.call-update) | async-done | bytes 1048592 | tf_op jit(solution)/shard_map/all_gather | solution.py:23
  20.7 2.7 convolution_bitcast_fusion
  23.3 4.1 copy.30
  27.4 6.8 all-to-all-start
  34.3 159.2 %all-to-all-done = f32[1024,16,128]{2,0,1:T(8,128)} async-done(((f32[1024,16,128]{2,0,1:T(8,128)}), f32[1024,16,128]{2,0,1:T(8,128)}, u32[]{:S(2)}, u32[]{:S(2)}) %all-to-all-start) | async-done | bytes 8388640 | tf_op jit(solution)/shard_map/all_to_all | solution.py:27
  193.5 3.8 reduce_sum.18
  198.4 70.9 %psum.35 = f32[]{:T(128)} all-reduce(f32[]{:T(128)} %fusion.10), channel_id=1, replica_groups=mesh['tok'=16,'blk'=2] {'tok','blk'}, use_global_device_ids=true, to_apply=%region_2.3 | all-reduce | flops 1 | bytes 8 | tf_op jit(solution)/shard_map/psum | solution.py:36
  270.9 110.8 %all-reduce.5.cloned.1.call-done = f32[1024,128]{0,1:T(8,128)} async-done(((f32[1024,128]{0,1:T(8,128)}), f32[1024,128]{0,1:T(8,128)}) %all-reduce.5.cloned.1.call-update) | async-done | bytes 524304 | tf_op jit(solution)/shard_map/psum | solution.py:11
  381.8 9.5 %all-gather.8.cloned.1.call-done = f32[2048,128]{0,1:T(8,128)} async-done(((f32[1024,128]{0,1:T(8,128)}), f32[2048,128]{0,1:T(8,128)}) %all-gather.8.cloned.1.call-update) | async-done | bytes 1048592 | tf_op jit(solution)/shard_map/all_gather | solution.py:41
  393.1 11.7 %cholesky.74 = f32[128,128]{1,0:T(8,128)S(1)} custom-call(f32[128,128]{1,0:T(8,128)S(1)} %fusion.28), custom_call_target="Cholesky" | custom-call | tf_op jit(solution)/shard_map/jit(cholesky)/cholesky | solution.py:43
  406.1 9.8 %custom-call.8 = f32[1,128,128]{1,2,0:T(8,128)S(1)} custom-call(f32[1,128,128]{2,1,0:T(8,128)S(1)} %fusion.17), custom_call_target="InvertDiagBlocksLowerTriangular" | custom-call | tf_op jit(solution)/shard_map/jit(_solve_triangular)/triangular_solve | solution.py:44
  416.0 2.3 fusion.8
  419.8 110.4 %all-reduce.7.cloned.1.call-done = f32[1024,128]{0,1:T(8,128)} async-done(((f32[1024,128]{0,1:T(8,128)}), f32[1024,128]{0,1:T(8,128)}) %all-reduce.7.cloned.1.call-update) | async-done | bytes 524304 | tf_op jit(solution)/shard_map/psum | solution.py:11
  530.4 9.2 %all-gather.10.cloned.1.call-done = f32[2048,128]{0,1:T(8,128)} async-done(((f32[1024,128]{0,1:T(8,128)}), f32[2048,128]{0,1:T(8,128)}) %all-gather.10.cloned.1.call-update) | async-done | bytes 1048592 | tf_op jit(solution)/shard_map/all_gather | solution.py:41
  541.4 11.7 %cholesky.85 = f32[128,128]{1,0:T(8,128)S(1)} custom-call(f32[128,128]{1,0:T(8,128)S(1)} %fusion.26), custom_call_target="Cholesky" | custom-call | tf_op jit(solution)/shard_map/jit(cholesky)/cholesky | solution.py:43
  554.5 9.8 %custom-call.9 = f32[1,128,128]{1,2,0:T(8,128)S(1)} custom-call(f32[1,128,128]{2,1,0:T(8,128)S(1)} %fusion.18), custom_call_target="InvertDiagBlocksLowerTriangular" | custom-call | tf_op jit(solution)/shard_map/jit(_solve_triangular)/triangular_solve | solution.py:44
  568.1 110.4 %all-reduce.9.cloned.1.call-done = f32[1024,128]{0,1:T(8,128)} async-done(((f32[1024,128]{0,1:T(8,128)}), f32[1024,128]{0,1:T(8,128)}) %all-reduce.9.cloned.1.call-update) | async-done | bytes 524304 | tf_op jit(solution)/shard_map/psum | solution.py:11
  678.8 9.3 %all-gather.12.cloned.1.call-done = f32[2048,128]{0,1:T(8,128)} async-done(((f32[1024,128]{0,1:T(8,128)}), f32[2048,128]{0,1:T(8,128)}) %all-gather.12.cloned.1.call-update) | async-done | bytes 1048592 | tf_op jit(solution)/shard_map/all_gather | solution.py:41
  689.9 11.7 %cholesky.96 = f32[128,128]{1,0:T(8,128)S(1)} custom-call(f32[128,128]{1,0:T(8,128)S(1)} %fusion.24), custom_call_target="Cholesky" | custom-call | tf_op jit(solution)/shard_map/jit(cholesky)/cholesky | solution.py:43
  703.0 9.8 %custom-call.10 = f32[1,128,128]{1,2,0:T(8,128)S(1)} custom-call(f32[1,128,128]{2,1,0:T(8,128)S(1)} %fusion.19), custom_call_target="InvertDiagBlocksLowerTriangular" | custom-call | tf_op jit(solution)/shard_map/jit(_solve_triangular)/triangular_solve | solution.py:44
  716.8 110.1 %all-reduce.11.cloned.1.call-done = f32[1024,128]{0,1:T(8,128)} async-done(((f32[1024,128]{0,1:T(8,128)}), f32[1024,128]{0,1:T(8,128)}) %all-reduce.11.cloned.1.call-update) | async-done | bytes 524304 | tf_op jit(solution)/shard_map/psum | solution.py:11
  827.0 9.6 %all-gather.14.cloned.1.call-done = f32[2048,128]{0,1:T(8,128)} async-done(((f32[1024,128]{0,1:T(8,128)}), f32[2048,128]{0,1:T(8,128)}) %all-gather.14.cloned.1.call-update) | async-done | bytes 1048592 | tf_op jit(solution)/shard_map/all_gather | solution.py:41
  838.4 11.7 %cholesky.107 = f32[128,128]{1,0:T(8,128)S(1)} custom-call(f32[128,128]{1,0:T(8,128)S(1)} %fusion.22), custom_call_target="Cholesky" | custom-call | tf_op jit(solution)/shard_map/jit(cholesky)/cholesky | solution.py:43
  851.4 9.8 %custom-call.11 = f32[1,128,128]{1,2,0:T(8,128)S(1)} custom-call(f32[1,128,128]{2,1,0:T(8,128)S(1)} %fusion.20), custom_call_target="InvertDiagBlocksLowerTriangular" | custom-call | tf_op jit(solution)/shard_map/jit(_solve_triangular)/triangular_solve | solution.py:44
  (58 shorter events, 29.2 us)
Async XLA Ops:
  6.5 14.1 %all-gather.6.cloned.1.call-start = ((), (), s32[]{:S(2)}) async-start(), calls=%async_computation.1 | async-start | bytes 1572864 | tf_op jit(solution)/shard_map/all_gather | solution.py:23
  27.4 166.1 %all-to-all-start = ((f32[1024,16,128]{2,0,1:T(8,128)}), f32[1024,16,128]{2,0,1:T(8,128)}, u32[]{:S(2)}, u32[]{:S(2)}) async-start(f32[1024,16,128]{2,0,1:T(8,128)} %bitcast.71), calls=%async_computation | async-start | bytes 16777216 | tf_op jit(solution)/shard_map/all_to_all | solution.py:27
  34.2 347.4 %all-reduce.5.cloned.1.call-start = ((), (), s32[]{:S(2)}) async-start(), calls=%async_computation.2 | async-start | bytes 1048576 | tf_op jit(solution)/shard_map/psum | solution.py:11
  270.9 120.4 %all-gather.8.cloned.1.call-start = ((), (), s32[]{:S(2)}) async-start(), calls=%async_computation.3 | async-start | bytes 1572864 | tf_op jit(solution)/shard_map/all_gather | solution.py:41
  381.7 148.5 %all-reduce.7.cloned.1.call-start = ((), (), s32[]{:S(2)}) async-start(), calls=%async_computation.4 | async-start | bytes 1048576 | tf_op jit(solution)/shard_map/psum | solution.py:11
  419.8 119.9 %all-gather.10.cloned.1.call-start = ((), (), s32[]{:S(2)}) async-start(), calls=%async_computation.5 | async-start | bytes 1572864 | tf_op jit(solution)/shard_map/all_gather | solution.py:41
  530.2 148.3 %all-reduce.9.cloned.1.call-start = ((), (), s32[]{:S(2)}) async-start(), calls=%async_computation.6 | async-start | bytes 1048576 | tf_op jit(solution)/shard_map/psum | solution.py:11
  568.0 120.1 %all-gather.12.cloned.1.call-start = ((), (), s32[]{:S(2)}) async-start(), calls=%async_computation.7 | async-start | bytes 1572864 | tf_op jit(solution)/shard_map/all_gather | solution.py:41
  678.5 148.5 %all-reduce.11.cloned.1.call-start = ((), (), s32[]{:S(2)}) async-start(), calls=%async_computation.8 | async-start | bytes 1048576 | tf_op jit(solution)/shard_map/psum | solution.py:11
  716.5 120.1 %all-gather.14.cloned.1.call-start = ((), (), s32[]{:S(2)}) async-start(), calls=%async_computation.9 | async-start | bytes 1572864 | tf_op jit(solution)/shard_map/all_gather | solution.py:41
Sparse Core Ops, SparseCore 0:
  8.9 11.7 all-gather.5
  271.0 110.6 all-reduce.4
  383.2 8.0 all-gather.7
  419.9 110.2 all-reduce.6
  531.6 8.0 all-gather.9
  568.2 110.2 all-reduce.8
  680.0 8.0 all-gather.11
  716.6 110.2 all-reduce.10
  828.5 8.0 all-gather.13
where the time goes:
time: 873 us; the launch traced here: 872 us
  waiting for transfers between devices  653 us (75%)
  other arithmetic  100 us (11%)
  blocking collectives  70.9 us (8%)
  matrix products  16.8 us (2%)
  between operations  14.1 us (2%)
  local copies, waits for them, and re-layouts  8.97 us (1%)
    psum x4, waiting for transfers between devices, spread(): return lax.psum(block, axis)  442 us
    all_to_all x1, waiting for transfers between devices, shards(): lax.all_to_all(partial_rows, 'tok', split_axis=1, concat_axis=0, tiled=True)  159 us
    psum x1, blocking collectives, shards(): lax.psum(jnp.sum(jnp.where(on_diag, hessian_tile, 0.0)), ('tok', 'blk'))  70.9 us
    another operation x12, other arithmetic, shards(): factor = jnp.linalg.cholesky(pivot_block)  49.6 us
    another operation x8, other arithmetic, shards(): solved = jax.scipy.linalg.solve_triangular(factor, column.T, lower=True).T  41.9 us
    all_gather x4, waiting for transfers between devices, shards(): column = lax.all_gather(strip_rows, 'blk', axis=0, tiled=True)  37.6 us
  transfers between devices with their start and end apart: 10, of which 10 were waited for; matrix products, arithmetic and copies ran while one was open for 0% of the time, Pallas kernels for 0%

commit v1 on v0

v1 whole, which is shorter than its diff:
```python
import functools
import jax
import jax.numpy as jnp
from jax import lax
from jax.experimental import pallas as pl
from jax.experimental.pallas import tpu as pltpu
from jax.sharding import PartitionSpec as P

STEPS = 4
GROUP = 8
HIGH = lax.Precision.HIGHEST


def factor_block(block):
    size = block.shape[0]
    count = size // GROUP
    shape = (GROUP, size)
    lanes = lax.broadcasted_iota(jnp.int32, shape, 1)
    subs = lax.broadcasted_iota(jnp.int32, shape, 0)
    left = [block[GROUP * g : GROUP * (g + 1), :] for g in range(count)]
    right = [jnp.where(lanes == subs + GROUP * g, 1.0, 0.0) for g in range(count)]

    def column(rows, j):
        return jnp.broadcast_to(rows[:, j : j + 1], shape)

    def row(rows, i):
        return jnp.broadcast_to(rows[i : i + 1, :], shape)

    for g in range(count):
        base = GROUP * g
        cols = [column(left[g], base + j) for j in range(GROUP)]
        a = [[row(cols[j], i) for j in range(i + 1)] for i in range(GROUP)]
        low = [[None] * GROUP for _ in range(GROUP)]
        inv = [None] * GROUP
        for j in range(GROUP):
            inv[j] = lax.rsqrt(a[j][j])
            for i in range(j + 1, GROUP):
                low[i][j] = a[i][j] * inv[j]
            for i in range(j + 1, GROUP):
                for m in range(j + 1, i + 1):
                    a[i][m] = a[i][m] - low[i][j] * low[m][j]
        r_left = [row(left[g], i) for i in range(GROUP)]
        r_right = [row(right[g], i) for i in range(GROUP)]
        u_left, u_right = [], []
        for i in range(GROUP):
            for rows, done in ((r_left, u_left), (r_right, u_right)):
                total = rows[i]
                for m in range(i):
                    total = total - low[i][m] * done[m]
                done.append(total * inv[i])
        g_left, g_right = [None] * GROUP, [None] * GROUP
        for i in reversed(range(GROUP)):
            for rows, done in ((u_left, g_left), (u_right, g_right)):
                total = rows[i]
                for m in range(i + 1, GROUP):
                    total = total - low[m][i] * done[m]
                done[i] = total * inv[i]
        out_left, out_right = u_left[0], u_right[0]
        for i in range(1, GROUP):
            out_left = jnp.where(subs == i, u_left[i], out_left)
            out_right = jnp.where(subs == i, u_right[i], out_right)
        for h in range(g + 1, count):
            rows = [column(left[h], base + j) for j in range(GROUP)]
            for j in range(GROUP):
                left[h] = left[h] - rows[j] * g_left[j]
                right[h] = right[h] - rows[j] * g_right[j]
        left[g], right[g] = out_left, out_right
    return jnp.concatenate(left, 0), jnp.concatenate(right, 0)


def factor_kernel(width, a_ref, u_ref, m_ref):
    n = a_ref.shape[0]
    m_ref[:, :n] = a_ref[...]
    ids = lax.broadcasted_iota(jnp.int32, (n, n), 0) == lax.broadcasted_iota(jnp.int32, (n, n), 1)
    m_ref[:, n:] = jnp.where(ids, 1.0, 0.0)

    for k in range(n // width):
        at = k * width
        _, inverse = factor_block(m_ref[at : at + width, at : at + width])
        upper = jnp.dot(inverse, m_ref[at : at + width, :], precision=HIGH, preferred_element_type=jnp.float32)
        col_ids = lax.broadcasted_iota(jnp.int32, upper.shape, 1)
        row_ids = lax.broadcasted_iota(jnp.int32, upper.shape, 0) + at
        upper = jnp.where((col_ids >= row_ids) & (col_ids <= row_ids + n), upper, 0.0)
        u_ref[at : at + width, :] = upper
        if at + width < n:
            m_ref[at + width :, :] -= lax.dot_general(
                upper[:, at + width : n], upper, (((0,), (0,)), ((), ())),
                precision=HIGH, preferred_element_type=jnp.float32,
            )


def factor(a):
    n = a.shape[0]
    width = min(128, n)
    out = pl.pallas_call(
        functools.partial(factor_kernel, width),
        out_shape=jax.ShapeDtypeStruct((n, 2 * n), jnp.float32),
        in_specs=[pl.BlockSpec(memory_space=pltpu.VMEM)],
        out_specs=pl.BlockSpec(memory_space=pltpu.VMEM),
        scratch_shapes=[pltpu.VMEM((n, 2 * n), jnp.float32)],
        compiler_params=pltpu.CompilerParams(vmem_limit_bytes=48 * 1024 * 1024),
    )(a)
    return out[:, :n], out[:, n:]


def gram(a, b):
    return lax.dot_general(a, b, (((0,), (0,)), ((), ())), preferred_element_type=jnp.float32)


def spread(block, holder):
    return lax.psum(jnp.where(lax.axis_index("blk") == holder, block, 0), "blk")


def gather(activations, lead, strip_width):
    rows_block = activations.shape[1]
    tok_index = lax.axis_index("tok")
    own = lax.all_gather(activations, "tok", axis=0, tiled=True)
    start = tok_index * strip_width
    strip = lax.dynamic_slice_in_dim(own, lax.rem(start, rows_block), strip_width, 1)
    if lax.axis_size("blk") > 2:
        first = spread(own[:, :lead], 0)
        strip = spread(strip, start // rows_block)
    else:
        both = lax.all_gather(jnp.concatenate([own[:, :lead], strip], 1), "blk", axis=0)
        first = both[0, :, :lead]
        strip = lax.dynamic_index_in_dim(both, start // rows_block, 0, False)[:, lead:]
    square = jnp.sum(jnp.square(own.astype(jnp.float32)))
    squares = jnp.sum(lax.all_gather(jnp.broadcast_to(square, (8, 128)), "blk", axis=0)[:, 0, 0])
    return own, first, strip, squares


def finish(own, first, strip, squares, sizes):
    rows_block, full_width, strip_width, lead, total_tokens = sizes
    tok_index = lax.axis_index("tok")
    blk_index = lax.axis_index("blk")
    scale = 2.0 / total_tokens
    damping = 0.01 * squares * scale / full_width
    corner = gram(first, first) * scale
    ids = jnp.arange(lead, dtype=jnp.int32)
    corner = corner + jnp.where(ids[:, None] == ids[None, :], damping, 0.0)
    upper, inverse = factor(corner)
    side = gram(own, first) * scale
    tile = gram(own, strip) * scale
    cross = gram(strip, first) * scale
    lower_rows = lax.dot_general(side, inverse, (((1,), (1,)), ((), ())), precision=HIGH)
    lower_cols = lax.dot_general(cross, inverse, (((1,), (1,)), ((), ())), precision=HIGH)
    row_ids = blk_index * rows_block + jnp.arange(rows_block, dtype=jnp.int32)[:, None]
    col_ids = tok_index * strip_width + jnp.arange(strip_width, dtype=jnp.int32)[None, :]
    schur = tile + jnp.where(row_ids == col_ids, damping, 0.0)
    schur = schur - lax.dot_general(lower_rows, lower_cols, (((1,), (1,)), ((), ())), precision=HIGH)
    at = jnp.minimum(tok_index * strip_width, lead - strip_width)
    leading = jnp.concatenate([upper.T, jnp.zeros((max(rows_block - lead, 0), lead), jnp.float32)], 0)
    head = jnp.where(row_ids < lead, leading, lower_rows)
    head = lax.dynamic_slice_in_dim(head, at, strip_width, 1)
    result = jnp.where(col_ids < lead, head, schur)
    return jnp.where((row_ids >= col_ids) & ((row_ids >= lead) | (col_ids < lead)), result, 0.0)


def shards(activations):
    rows_block = activations.shape[1]
    tok_count = lax.axis_size("tok")
    full_width = rows_block * lax.axis_size("blk")
    strip_width = full_width // tok_count
    lead = STEPS * strip_width
    total_tokens = activations.shape[0] * tok_count
    sizes = (rows_block, full_width, strip_width, lead, total_tokens)
    return finish(*gather(activations, lead, strip_width), sizes)


def solution(mesh):
    return jax.shard_map(
        shards,
        mesh=mesh,
        in_specs=(P("tok", "blk"),),
        out_specs=P("blk", "tok"),
        check_vma=False,
    )
```

time: 873 us -> 232 us (0.27)
  waiting for transfers between devices: 653 us -> 124 us
  other arithmetic: 100 us -> 12 us
  blocking collectives: 70.9 us -> 2.63 us
  Pallas kernels: 0 us -> 25.5 us
  matrix products: 16.8 us -> 31.9 us
    psum x4 -> x0, waiting for transfers between devices: 442 us -> none  [spread(): return lax.psum(block, axis)]
    all_to_all x1 -> x0, waiting for transfers between devices: 159 us -> none  [shards(): lax.all_to_all(partial_rows, 'tok', split_axis=1, concat_axis=0, tiled=True)]
    another operation x20 -> x0, other arithmetic: 91.4 us -> none  [the longest x12 49.6 us: shards(): factor = jnp.linalg.cholesky(pivot_block)]
    all_gather x5 -> x2, waiting for transfers between devices: 51 us -> 124 us  [the longest x1 118 us: gather(): own = lax.all_gather(activations, 'tok', axis=0, tiled=True)]
    psum x1 -> x0, blocking collectives: 70.9 us -> none  [shards(): lax.psum(jnp.sum(jnp.where(on_diag, hessian_tile, 0.0)), ('tok', 'blk'))]
    pallas_call x0 -> x1, Pallas kernels: none -> 25.5 us  [factor(): pl.pallas_call(functools.partial(factor_kernel, width), out_shape=jax.Sha...]
    dot_general x5 -> x7, matrix products: 7.8 us -> 31.9 us  [the longest x4 20.9 us: gram(): lax.dot_general(a, b, (((0,), (0,)), ((), ())), preferred_element_type=jn...]
    another operation x4 -> x0, matrix products: 9.03 us -> none  [shards(): solved = jax.scipy.linalg.solve_triangular(factor, column.T, lower=True).T]
  transfers between devices with their start and end apart: 10 -> 2, of which waited for: 10 -> 2; matrix products, arithmetic and copies ran while one was open for 0% -> 5% of each run, Pallas kernels for 0% -> 0%
where the time goes in v1:
time: 232 us; the launch traced here: 228 us
  waiting for transfers between devices  124 us (53%)
  matrix products  31.9 us (14%)
  Pallas kernels  25.5 us (11%)
  local copies, waits for them, and re-layouts  17 us (7%)
  between operations  14.7 us (6%)
  other arithmetic  12 us (5%)
  blocking collectives  2.63 us (1%)
    all_gather x1, waiting for transfers between devices, gather(): own = lax.all_gather(activations, 'tok', axis=0, tiled=True)  118 us
    pallas_call x1, Pallas kernels, factor(): pl.pallas_call(functools.partial(factor_kernel, width), out_shape=jax.Sha...  25.5 us
    dot_general x4, matrix products, gram(): lax.dot_general(a, b, (((0,), (0,)), ((), ())), preferred_element_type=jn...  20.9 us
    reduce_sum x1, other arithmetic, gather(): square = jnp.sum(jnp.square(own.astype(jnp.float32)))  8.65 us
    dot_general x1, matrix products, finish(): lax.dot_general(side, inverse, (((1,), (1,)), ((), ())), precision=HIGH)  6.69 us
    all_gather x1, waiting for transfers between devices, gather(): lax.all_gather(jnp.concatenate([own[:, :lead], strip], 1), 'blk', axis=0)  5.73 us
    squeeze x1, local copies, waits for them, and re-layouts, gather(): lax.dynamic_index_in_dim(both, start // rows_block, 0, False)[:, lead:]  5.4 us
    unnamed x12, local copies, waits for them, and re-layouts  4.7 us
  transfers between devices with their start and end apart: 2, of which 2 were waited for; matrix products, arithmetic and copies ran while one was open for 5% of the time, Pallas kernels for 0%

profile of v1, /device:TPU:0, one launch (start us, length us, event | category | flops | bytes accessed | tf_op | source)
XLA Modules:
  0.0 228.1 jit_solution(6713341250457988477)
XLA Ops:
  6.5 0.7 all-gather.4.cloned.1.call-update
  7.3 117.8 %all-gather.4.cloned.1.call-done = bf16[4096,1024]{1,0:T(8,128)(2,1)} async-done(((bf16[256,1024]{1,0:T(8,128)(2,1)}), bf16[4096,1024]{1,0:T(8,128)(2,1)}) %all-gather.4.cloned.1.call-update) | async-done | bytes 8388624 | tf_op jit(solution)/shard_map/all_gather | solution.py:117
  125.2 2.5 %slice.24 = bf16[4096,512]{1,0:T(8,128)(2,1)S(1)} slice(bf16[4096,1024]{1,0:T(8,128)(2,1)} %all-gather.4.cloned.1.call-done), slice={[0:4096], [0:512]} | slice | bytes 8388608 | tf_op jit(solution)/shard_map/slice | solution.py:124
  127.6 1.3 constant_dynamic-slice_fusion.1
  128.9 2.8 %pad_maximum_fusion = bf16[4096,640]{1,0:T(8,128)(2,1)} fusion(bf16[4096,128]{1,0:T(8,128)(2,1)S(1)} %constant_dynamic-slice_fusion.1, bf16[4096,512]{1,0:T(8,128)(2,1)S(1)} %slice.24), kind=kLoop, calls=%fused_computation.1 | loop fusion | flops 10485760 | bytes 10485760 | tf_op jit(solution)/shard_map/concatenate | solution.py:124
  131.7 0.6 copy-done.1
  132.3 0.6 dynamic-slice
  133.0 8.6 %multiply_reduce_fusion = f32[]{:T(128)} fusion(bf16[4096,1024]{1,0:T(8,128)(2,1)} %all-gather.4.cloned.1.call-done), kind=kLoop, calls=%fused_computation | loop fusion | flops 12582911 | bytes 8388612 | tf_op jit(solution)/shard_map/reduce_sum | solution.py:127
  141.7 1.4 dynamic-update-slice
  143.1 2.6 %all-reduce.1 = f32[2]{0:T(128)S(1)} all-reduce(f32[2]{0:T(128)S(1)} %dynamic-update-slice), channel_id=2, replica_groups=mesh['tok'=16,'blk'=2] {'blk'}, use_global_device_ids=true, to_apply=%add.1 | all-reduce | flops 2 | bytes 16
  145.7 0.6 reduce_sum.19
  147.0 5.7 %all-gather.6.cloned.1.call-done = bf16[8192,640]{1,0:T(8,128)(2,1)} async-done(((bf16[4096,640]{1,0:T(8,128)(2,1)}), bf16[8192,640]{1,0:T(8,128)(2,1)}) %all-gather.6.cloned.1.call-update) | async-done | bytes 10485776 | tf_op jit(solution)/shard_map/all_gather | solution.py:124
  152.7 5.4 %dynamic-slice_bitcast_fusion = bf16[4096,640]{1,0:T(8,128)(2,1)} fusion(bf16[2,4096,640]{2,1,0:T(8,128)(2,1)} %bitcast.29, s32[]{:T(128)S(6)} %select_n.40), kind=kLoop, calls=%fused_computation.2 | loop fusion | bytes 10485764 | tf_op jit(solution)/shard_map/jit(dynamic_index_in_dim)/squeeze | solution.py:126
  158.1 6.0 %fusion.6.a_ref = f32[512,512]{1,0:T(8,128)S(1)} fusion(bf16[2,4096,640]{2,1,0:T(8,128)(2,1)} %bitcast.30, f32[]{:T(128)S(6)} %div.11), kind=kOutput, calls=%fused_computation.11 | convolution fusion | flops 2148532224 | bytes 5242884 | tf_op jit(solution)/shard_map/dot_general | solution.py:107
  164.1 25.5 %shard_map.17 = f32[512,1024]{1,0:T(8,128)S(1)} custom-call(f32[512,512]{1,0:T(8,128)S(1)} %fusion.6.a_ref), custom_call_target="tpu_custom_call" | custom-call | tf_op jit(solution)/shard_map/pallas_call | solution.py:95
  189.7 6.6 %fusion.1 = f32[512,1024]{1,0:T(8,128)S(1)} fusion(bf16[4096,1024]{1,0:T(8,128)(2,1)S(1)} %bitcast.28, bf16[2,4096,640]{2,1,0:T(8,128)(2,1)} %bitcast.31), kind=kOutput, calls=%fused_computation.5 | convolution fusion | flops 4294967296 | bytes 14680064 | tf_op jit(solution)/shard_map/dot_general | solution.py:107
  196.3 6.7 %fusion.3 = f32[1024,512]{1,0:T(8,128)S(1)} fusion(f32[512,1024]{1,0:T(8,128)S(1)} %fusion.1, f32[512,1024]{1,0:T(8,128)S(1)} %shard_map.17), kind=kOutput, calls=%fused_computation.7 | convolution fusion | flops 3221749760 | bytes 5242880 | tf_op jit(solution)/shard_map/dot_general | solution.py:145
  203.0 3.3 %fusion.11 = f32[128,512]{1,0:T(8,128)S(1)} fusion(bf16[2,4096,640]{2,1,0:T(8,128)(2,1)} %bitcast.32, bf16[4096,640]{1,0:T(8,128)(2,1)} %dynamic-slice_bitcast_fusion), kind=kOutput, calls=%fused_computation.18 | convolution fusion | flops 536936448 | bytes 5505024 | tf_op jit(solution)/shard_map/dot_general | solution.py:107
  206.2 1.2 fusion.13
  207.4 1.0 constant_dynamic-slice_fusion
  208.4 2.0 copy.6
  210.5 5.1 %fusion.10 = f32[1024,128]{0,1:T(8,128)S(1)} fusion(bf16[4096,1024]{1,0:T(8,128)(2,1)} %all-gather.4.cloned.1.call-done, bf16[4096,640]{1,0:T(8,128)(2,1)} %dynamic-slice_bitcast_fusion, f32[]{:T(128)S(6)} %div.11, s32[1024]{0:T(1024)S(1)} %iota_add_fusion, s32[128]{0:T(128)S(1)} %iota_add_fusion.1), kind=kOutput, calls=%fused_computation.17 | convolution fusion | flops 1074266112 | bytes 9966084 | tf_op jit(solution)/shard_map/dot_general | solution.py:107
  215.6 3.2 %fusion.9 = f32[1024,128]{0,1:T(8,128)} fusion(f32[1024,128]{0,1:T(8,128)S(1)} %fusion.10, f32[1024,512]{1,0:T(8,128)S(1)} %fusion.3, f32[128,512]{1,0:T(8,128)S(1)} %fusion.13, f32[1024,128]{0,1:T(8,128)S(1)} %copy-done, s32[]{:T(128)S(6)} %select_n.38, f32[512,512]{0,1:T(8,128)S(1)} %slice_bitcast_fusion.10, s32[1024]{0:T(1024)S(1)} %iota_add_fusion, ...), kind=kOutput, calls=%fused_computation.16 | convolution fusion | flops 806223872 | bytes 4987524 | tf_op jit(solution)/shard_map/dot_general | solution.py:150
  218.7 2.0 copy.4
  (17 shorter events, 0.2 us)
Async XLA Ops:
  6.5 118.6 %all-gather.4.cloned.1.call-start = ((), (), s32[]{:S(2)}) async-start(), calls=%async_computation | async-start | bytes 8912896 | tf_op jit(solution)/shard_map/all_gather | solution.py:117
  7.3 145.4 %all-gather.6.cloned.1.call-start = ((), (), s32[]{:S(2)}) async-start(), calls=%async_computation.1 | async-start | bytes 15728640 | tf_op jit(solution)/shard_map/all_gather | solution.py:124
  131.7 0.7 copy-start.1
  152.7 37.0 %slice-start = ((s8[8388608]{0:T(1024)(128)(4,1)}), s8[4194304]{0:T(1024)(128)(4,1)S(1)}, s32[]{:S(2)}) async-start(s8[8388608]{0:T(1024)(128)(4,1)} %bitcast.27), calls=%async_computation.2 | async-start | bytes 8388608
  158.1 31.6 %slice-start.1 = ((s8[8388608]{0:T(1024)(128)(4,1)}), s8[4194304]{0:T(1024)(128)(4,1)S(1)}, s32[]{:S(2)}) async-start(s8[8388608]{0:T(1024)(128)(4,1)} %bitcast.27), calls=%async_computation.3 | async-start | bytes 8388608
  210.5 5.1 %copy-start = (f32[1024,128]{0,1:T(8,128)S(1)}, f32[1024,128]{0,1:T(8,128)}, u32[]{:S(2)}) copy-start(f32[1024,128]{0,1:T(8,128)} %copy.6) | copy-start | bytes 1572868
Sparse Core Ops, SparseCore 0:
  10.1 115.0 all-gather.3
  131.8 20.8 all-gather.5

commit v2 on v1

--- a/solution.py
+++ b/solution.py
@@ -129,6 +129,201 @@
     return own, first, strip, squares
 
 
+ORDERS = ("zyx", "zxy", "xzy", "yzx")
+SIZES = {"z": 4, "y": 2, "x": 2}
+
+
+def gather_kernel(lead, strip_width, act_ref, sq_in, own_ref, first_ref, strip_ref, sq_ref,
+                  send, recv, push_send, push_recv, sq_send, sq_recv, local):
+    tok = lax.axis_index("tok")
+    blk = lax.axis_index("blk")
+    count = lax.axis_size("tok")
+    blks = lax.axis_size("blk")
+    rows = act_ref.shape[0] // len(ORDERS)
+    z, y, x = tok // 4, lax.rem(tok // 2, 2), lax.rem(tok, 2)
+    me = tok * blks + blk
+    total = count * blks
+
+    barrier = pltpu.get_barrier_semaphore()
+
+    def peer(i):
+        other = lax.rem(me + i, total)
+        return (other // blks, lax.rem(other, blks))
+
+    def greet(i, carry):
+        pl.semaphore_signal(barrier, inc=1, device_id=peer(i), device_id_type=pl.DeviceIdType.MESH)
+        return carry
+
+    lax.fori_loop(1, total, greet, 0)
+    own_copy = pltpu.make_async_copy(act_ref, own_ref.at[tok], local.at[0])
+    sq_copy = pltpu.make_async_copy(sq_in, sq_ref.at[me], local.at[1])
+    own_copy.start()
+    sq_copy.start()
+    pl.semaphore_wait(barrier, total - 1)
+
+    def index(dz, dy, dx):
+        return (z + dz) * 4 + lax.rem(y + dy, 2) * 2 + lax.rem(x + dx, 2)
+
+    def part(c):
+        return pl.ds(c * rows, rows)
+
+    def link(c, src, way, own):
+        step = {"z+": (1, 0, 0), "z-": (-1, 0, 0), "y": (0, 1, 0), "x": (0, 0, 1)}[way]
+        slot = ("z+", "z-", "y", "x").index(way)
+        source = act_ref.at[part(c)] if own else own_ref.at[src, part(c)]
+        return pltpu.make_async_remote_copy(
+            src_ref=source,
+            dst_ref=own_ref.at[src, part(c)],
+            send_sem=send.at[c, slot, src],
+            recv_sem=recv.at[c, src],
+            device_id=(index(*step), blk),
+            device_id_type=pl.DeviceIdType.MESH,
+        )
+
+    def ways(order, delta):
+        last = -1
+        for s, dim in enumerate(order):
+            if delta["zyx".index(dim)]:
+                last = s
+        result = []
+        for s, dim in enumerate(order):
+            if s > last:
+                result += ["z+", "z-"] if dim == "z" else [dim]
+            elif s == last and dim == "z":
+                result += ["z+"] if delta[0] < 0 else ["z-"]
+        return result
+
+    def guarded(way, body):
+        if way == "z+":
+            pl.when(z < 3)(body)
+        elif way == "z-":
+            pl.when(z > 0)(body)
+        else:
+            body()
+
+    events = [(abs(dz) + dy + dx, c, (dz, dy, dx))
+              for dz in range(-3, 4) for dy in range(2) for dx in range(2)
+              for c in range(len(ORDERS))]
+    events.sort(key=lambda e: (e[0], abs(e[2][0]), e[1]))
+
+    def push(c, src, own):
+        source = act_ref if own else own_ref.at[src]
+        start = pl.multiple_of(lax.rem(tok * strip_width, act_ref.shape[1]), strip_width)
+        for k, (take, goal) in enumerate(((pl.ds(0, lead), first_ref), (pl.ds(start, strip_width), strip_ref))):
+            yield pltpu.make_async_remote_copy(
+                src_ref=source.at[part(c), take],
+                dst_ref=goal.at[src, part(c)],
+                send_sem=push_send.at[k],
+                recv_sem=push_recv.at[k],
+                device_id=(tok, 1 - blk),
+                device_id_type=pl.DeviceIdType.MESH,
+            )
+
+    def visit(event, wait):
+        _, c, delta = event
+        own = delta == (0, 0, 0)
+        src = index(*delta)
+        follow = ways(ORDERS[c], delta)
+
+        def run():
+            if wait:
+                for way in follow:
+                    guarded(way, lambda way=way: link(c, src, way, own).wait_send())
+                return
+            if not own:
+                link(c, src, "x", False).wait_recv()
+            for way in follow:
+                guarded(way, lambda way=way: link(c, src, way, own).start())
+
+            @pl.when(blk == 0)
+            def _():
+                for copy in push(c, src, own):
+                    copy.start()
+
+        if delta[0]:
+            pl.when((z + delta[0] >= 0) & (z + delta[0] <= 3))(run)
+        else:
+            run()
+
+    def sq_link(i):
+        return pltpu.make_async_remote_copy(
+            src_ref=sq_in,
+            dst_ref=sq_ref.at[me],
+            send_sem=sq_send.at[i],
+            recv_sem=sq_recv,
+            device_id=peer(i),
+            device_id_type=pl.DeviceIdType.MESH,
+        )
+
+    for event in events[: len(ORDERS)]:
+        visit(event, False)
+
+    def sq_start(i, carry):
+        sq_link(i).start()
+        return carry
+
+    lax.fori_loop(1, total, sq_start, 0)
+    for event in events[len(ORDERS):]:
+        visit(event, False)
+    for event in events:
+        visit(event, True)
+
+    def sq_wait(i, carry):
+        sq_link(i).wait_send()
+        return carry
+
+    lax.fori_loop(1, total, sq_wait, 0)
+    rest = sq_ref.at[pl.ds(0, total - 1)]
+    pltpu.make_async_copy(rest, rest, sq_recv).wait()
+    own_copy.wait()
+    sq_copy.wait()
+
+    @pl.when(blk == 0)
+    def _():
+        for k, goal in enumerate((first_ref, strip_ref)):
+            pltpu.make_async_copy(goal, goal, push_send.at[k]).wait()
+
+    @pl.when(blk == 1)
+    def _():
+        for k, goal in enumerate((first_ref, strip_ref)):
+            pltpu.make_async_copy(goal, goal, push_recv.at[k]).wait()
+
+
+def gather_links(activations, lead, strip_width):
+    rows, width = activations.shape
+    count = lax.axis_size("tok")
+    total = count * lax.axis_size("blk")
+    tok_index = lax.axis_index("tok")
+    blk_index = lax.axis_index("blk")
+    square = jnp.sum(jnp.square(activations.astype(jnp.float32)))
+    vmem = pl.BlockSpec(memory_space=pltpu.VMEM)
+    dma = pltpu.SemaphoreType.DMA
+    own, first, strip, squares = pl.pallas_call(
+        functools.partial(gather_kernel, lead, strip_width),
+        out_shape=[
+            jax.ShapeDtypeStruct((count, rows, width), activations.dtype),
+            jax.ShapeDtypeStruct((count, rows, lead), activations.dtype),
+            jax.ShapeDtypeStruct((count, rows, strip_width), activations.dtype),
+            jax.ShapeDtypeStruct((total, 8, 128), jnp.float32),
+        ],
+        in_specs=[vmem, vmem],
+        out_specs=[vmem] * 4,
+        scratch_shapes=[
+            dma((len(ORDERS), 4, count)), dma((len(ORDERS), count)),
+            dma((2,)), dma((2,)), dma((total,)), dma, dma((2,)),
+        ],
+        compiler_params=pltpu.CompilerParams(
+            collective_id=0, has_side_effects=True, vmem_limit_bytes=40 * 1024 * 1024
+        ),
+    )(activations, jnp.broadcast_to(square, (8, 128)))
+    own = own.reshape(count * rows, width)
+    first = jnp.where(blk_index == 0, own[:, :lead], first.reshape(count * rows, lead))
+    start = tok_index * strip_width
+    mine = lax.dynamic_slice_in_dim(own, lax.rem(start, width), strip_width, 1)
+    strip = jnp.where(blk_index == start // width, mine, strip.reshape(count * rows, strip_width))
+    return own, first, strip, jnp.sum(squares[:, 0, 0])
+
+
 def finish(own, first, strip, squares, sizes):
     rows_block, full_width, strip_width, lead, total_tokens = sizes
     tok_index = lax.axis_index("tok")
@@ -164,7 +359,8 @@
     lead = STEPS * strip_width
     total_tokens = activations.shape[0] * tok_count
     sizes = (rows_block, full_width, strip_width, lead, total_tokens)
-    return finish(*gather(activations, lead, strip_width), sizes)
+    gathered = gather_links if (tok_count, lax.axis_size("blk")) == (16, 2) else gather
+    return finish(*gathered(activations, lead, strip_width), sizes)
 
 
 def solution(mesh):

time: 232 us -> 142 us (0.61); the launches traced: 228 us -> 141 us
  waiting for transfers between devices: 124 us -> 0 us
  Pallas kernels: 25.5 us -> 102 us
  between operations: 14.7 us -> 0.78 us
  matrix products: 31.9 us -> 18.7 us
  local copies, waits for them, and re-layouts: 17 us -> 12 us
  other arithmetic: 12 us -> 8.33 us
  blocking collectives: 2.63 us -> 0 us
    all_gather x2 -> x0, waiting for transfers between devices: 124 us -> none  [the longest x1 118 us: gather(): own = lax.all_gather(activations, 'tok', axis=0, tiled=True)]
    pallas_call x0 -> x1, Pallas kernels: none -> 75.9 us  [gather_links(): pl.pallas_call(functools.partial(gather_kernel, lead, strip_width), out_s...]
    dot_general x4, matrix products: 20.9 us -> 9.76 us  [gram(): lax.dot_general(a, b, (((0,), (0,)), ((), ())), preferred_element_type=jn...]
    reduce_sum x2, other arithmetic: 9.25 us -> 2.55 us  [the longest x1 1.92 us: gather_links(): square = jnp.sum(jnp.square(activations.astype(jnp.float32)))]
    select_n x0 -> x2, other arithmetic: none -> 5.76 us  [the longest x1 4.04 us: gather_links(): jnp.where(blk_index == 0, own[:, :lead], first.reshape(count * rows, lead))]
    squeeze x1 -> x0, local copies, waits for them, and re-layouts: 5.4 us -> none  [gather(): lax.dynamic_index_in_dim(both, start // rows_block, 0, False)[:, lead:]]
    unnamed x12 -> x11, local copies, waits for them, and re-layouts: 4.7 us -> 8.26 us
    dot_general x1, matrix products: 6.69 us -> 3.48 us  [finish(): lax.dot_general(side, inverse, (((1,), (1,)), ((), ())), precision=HIGH)]
  transfers between devices with their start and end apart: 2 -> 0, of which waited for: 2 -> 0; matrix products, arithmetic and copies ran while one was open for 5% -> 0% of each run, Pallas kernels for 0% -> 0%
where the time goes in v2:
time: 142 us; the launch traced here: 141 us
  Pallas kernels  102 us (72%)
  matrix products  18.7 us (13%)
  local copies, waits for them, and re-layouts  12 us (8%)
  other arithmetic  8.33 us (6%)
    pallas_call x1, Pallas kernels, gather_links(): pl.pallas_call(functools.partial(gather_kernel, lead, strip_width), out_s...  75.9 us
    pallas_call x1, Pallas kernels, factor(): pl.pallas_call(functools.partial(factor_kernel, width), out_shape=jax.Sha...  25.7 us
    dot_general x4, matrix products, gram(): lax.dot_general(a, b, (((0,), (0,)), ((), ())), preferred_element_type=jn...  9.76 us
    unnamed x11, local copies, waits for them, and re-layouts  8.26 us
    dot_general x1, matrix products, finish(): lax.dot_general(lower_rows, lower_cols, (((1,), (1,)), ((), ())), precisi...  4.33 us
    select_n x1, other arithmetic, gather_links(): jnp.where(blk_index == 0, own[:, :lead], first.reshape(count * rows, lead))  4.04 us
    dot_general x1, matrix products, finish(): lax.dot_general(side, inverse, (((1,), (1,)), ((), ())), precision=HIGH)  3.48 us

profile of v2, /device:TPU:0, one launch (start us, length us, event | category | flops | bytes accessed | tf_op | source)
XLA Modules:
  0.0 141.5 jit_solution(15066473219668032607)
XLA Ops:
  0.0 1.9 %multiply_reduce_fusion = f32[]{:T(128)} fusion(bf16[256,1024]{1,0:T(8,128)(2,1)} %act_ref.1), kind=kLoop, calls=%fused_computation.16 | loop fusion | flops 786431 | bytes 524292 | tf_op jit(solution)/shard_map/reduce_sum | solution.py:298
  2.0 0.6 broadcast_in_dim.41.sq_in
  2.6 0.0 copy-start.2
  2.6 1.0 copy-done.2
  3.7 75.9 %shard_map.17 = (bf16[16,256,1024]{2,1,0:T(8,128)(2,1)S(1)}, bf16[16,256,512]{2,1,0:T(8,128)(2,1)S(1)}, bf16[16,256,128]{2,1,0:T(8,128)(2,1)S(1)}, f32[32,8,128]{2,1,0:T(8,128)S(1)}) custom-call(bf16[256,1024]{1,0:T(8,128)(2,1)S(1)} %copy-done.2, f32[8,128]{1,0:T(8,128)S(1)} %broadcast_in_dim.41.sq_in), custom_call_target="tpu_custom_call" | custom-call | tf_op jit(solution)/shard_map/pallas_call | solution.py:301
  79.6 1.9 %copy-done = bf16[16,256,512]{2,1,0:T(8,128)(2,1)} copy-done((bf16[16,256,512]{2,1,0:T(8,128)(2,1)}, bf16[16,256,512]{2,1,0:T(8,128)(2,1)S(1)}, u32[]{:S(2)}) %copy-start) | copy-done | bytes 4194328
  81.5 3.2 %copy-done.1 = bf16[16,256,1024]{2,1,0:T(8,128)(2,1)} copy-done((bf16[16,256,1024]{2,1,0:T(8,128)(2,1)}, bf16[16,256,1024]{2,1,0:T(8,128)(2,1)S(1)}, u32[]{:S(2)}) %copy-start.1) | copy-done | bytes 8388632
  84.7 0.6 slice_reduce_fusion
  86.0 0.0 slice-start
  86.0 1.7 %bitcast_select_fusion = bf16[4096,128]{1,0:T(8,128)(2,1)S(1)} fusion(bf16[16,256,128]{2,1,0:T(8,128)(2,1)S(1)} %get-tuple-element.12, bf16[4096,1024]{1,0:T(8,128)(2,1)} %bitcast.18, s32[]{:T(128)S(6)} %select_n.54, pred[]{:T(512)S(6)} %eq.32), kind=kLoop, calls=%fused_computation.13 | loop fusion | flops 524288 | bytes 3145733 | tf_op jit(solution)/shard_map/jit(_where)/select_n | solution.py:323
  87.7 4.0 %slice_select_fusion = bf16[4096,512]{1,0:T(8,128)(2,1)S(1)} fusion(bf16[4096,1024]{1,0:T(8,128)(2,1)} %bitcast.19, bf16[16,256,512]{2,1,0:T(8,128)(2,1)} %copy-done, pred[]{:T(512)S(6)} %eq.12), kind=kLoop, calls=%fused_computation | loop fusion | flops 2097152 | bytes 12582913 | tf_op jit(solution)/shard_map/jit(_where)/select_n | solution.py:320
  91.8 0.7 convolution_multiply_fusion.2
  92.5 0.0 slice-done.1
  92.6 2.1 %fusion.5 = f32[1024,128]{0,1:T(8,128)} fusion(bf16[4096,1024]{1,0:T(8,128)(2,1)S(1)} %bitcast.22, bf16[4096,128]{1,0:T(8,128)(2,1)S(1)} %bitcast_select_fusion, f32[]{:T(128)S(6)} %div.11, s32[1024]{0:T(1024)S(1)} %iota_add_fusion, s32[128]{0:T(128)S(1)} %iota_add_fusion.1), kind=kOutput, calls=%fused_computation.10 | convolution fusion | flops 1074266112 | bytes 9966084 | tf_op jit(solution)/shard_map/dot_general | solution.py:107
  94.7 4.5 %fusion.14 = f32[1024,512]{1,0:T(8,128)S(1)} fusion(bf16[4096,1024]{1,0:T(8,128)(2,1)S(1)} %bitcast.23, bf16[4096,512]{1,0:T(8,128)(2,1)S(1)} %slice_select_fusion), kind=kOutput, calls=%fused_computation.29 | convolution fusion | flops 4294967296 | bytes 14680064 | tf_op jit(solution)/shard_map/dot_general | solution.py:107
  99.2 2.4 %fusion.2.a_ref = f32[512,512]{1,0:T(8,128)S(1)} fusion(bf16[4096,512]{1,0:T(8,128)(2,1)S(1)} %slice_select_fusion, f32[]{:T(128)S(6)} %div.11), kind=kOutput, calls=%fused_computation.5 | convolution fusion | flops 2148532224 | bytes 5242884 | tf_op jit(solution)/shard_map/dot_general | solution.py:107
  101.6 25.7 %shard_map.18 = f32[512,1024]{1,0:T(8,128)S(1)} custom-call(f32[512,512]{1,0:T(8,128)S(1)} %fusion.2.a_ref), custom_call_target="tpu_custom_call" | custom-call | tf_op jit(solution)/shard_map/pallas_call | solution.py:95
  127.3 3.5 %fusion = f32[1024,512]{1,0:T(8,128)S(1)} fusion(f32[1024,512]{1,0:T(8,128)S(1)} %fusion.14, f32[512,1024]{1,0:T(8,128)S(1)} %shard_map.18), kind=kOutput, calls=%fused_computation.1 | convolution fusion | flops 3221749760 | bytes 5242880 | tf_op jit(solution)/shard_map/dot_general | solution.py:340
  130.8 1.2 fusion.7
  132.0 0.1 slice_bitcast_fusion
  132.1 1.0 constant_dynamic-slice_fusion
  133.1 2.0 %copy.8 = f32[1024,128]{0,1:T(8,128)} copy(f32[1024,128]{1,0:T(8,128)} %constant_dynamic-slice_fusion) | data formatting | bytes 1048576
  135.1 4.3 %fusion.4 = f32[1024,128]{0,1:T(8,128)} fusion(f32[1024,128]{0,1:T(8,128)} %fusion.5, f32[1024,512]{1,0:T(8,128)S(1)} %fusion, f32[128,512]{1,0:T(8,128)S(1)} %fusion.7, f32[1024,128]{0,1:T(8,128)} %copy.8, s32[]{:T(128)S(6)} %select_n.51, f32[512,512]{0,1:T(8,128)S(1)} %slice_bitcast_fusion, s32[1024]{0:T(1024)S(1)} %iota_add_fusion, ...), kind=kOutput, calls=%fused_computation.9 | convolution fusion | flops 806223872 | bytes 4987524 | tf_op jit(solution)/shard_map/dot_general | solution.py:345
  139.4 2.0 %copy.5 = f32[1024,128]{1,0:T(8,128)} copy(f32[1024,128]{0,1:T(8,128)} %fusion.4) | data formatting | bytes 1048576 | tf_op jit(solution)/shard_map/jit(_where)/select_n | solution.py:351
  (9 shorter events, 0.0 us)
Async XLA Ops:
  2.6 1.0 copy-start.2
  79.5 1.9 %copy-start = (bf16[16,256,512]{2,1,0:T(8,128)(2,1)}, bf16[16,256,512]{2,1,0:T(8,128)(2,1)S(1)}, u32[]{:S(2)}) copy-start(bf16[16,256,512]{2,1,0:T(8,128)(2,1)S(1)} %get-tuple-element.10) | copy-start | bytes 12582916
  81.5 3.2 %copy-start.1 = (bf16[16,256,1024]{2,1,0:T(8,128)(2,1)}, bf16[16,256,1024]{2,1,0:T(8,128)(2,1)S(1)}, u32[]{:S(2)}) copy-start(bf16[16,256,1024]{2,1,0:T(8,128)(2,1)S(1)} %get-tuple-element.9) | copy-start | bytes 25165828
  86.0 6.5 %slice-start = ((s8[8388608]{0:T(1024)(128)(4,1)}), s8[4194304]{0:T(1024)(128)(4,1)S(1)}, s32[]{:S(2)}) async-start(s8[8388608]{0:T(1024)(128)(4,1)} %bitcast.20), calls=%async_computation | async-start | bytes 8388608
  87.7 4.8 %slice-start.1 = ((s8[8388608]{0:T(1024)(128)(4,1)}), s8[4194304]{0:T(1024)(128)(4,1)S(1)}, s32[]{:S(2)}) async-start(s8[8388608]{0:T(1024)(128)(4,1)} %bitcast.20), calls=%async_computation.1 | async-start | bytes 8388608
